TPU v7x, 32 devices: a whole 2x2x4 slice. The times are simulated.
32 devices in a mesh: cp: 8 (over z, x), tp: 4 (over y, core).
Axes of the slice: x: 2, y: 2, z: 4, core: 2. Of those that a mesh axis runs over, the one named last changes fastest.
Arguments:
- tokens_in: bfloat16 [2048, 2048], P('cp'), may hold values from -6 to 6
- doc_ids: int32 [2048], P('cp'), may hold values from 0 to 3, never falling along the last dimension, each value on 1 to 1024 neighbouring positions
- expert_ids: int32 [2048, 2], P('cp'), may hold values from 0 to 7, all different within a row; in each aligned block of 256 rows (0 to 255, 256 to 511, ...) at most 96 rows name the same one
- attn_gain: bfloat16 [2048], P('cp'), may hold values from 0.099609375 to 1.8984375
- q_gain: bfloat16 [128], replicated, may hold values from 0.099609375 to 1.8984375
- k_gain: bfloat16 [128], replicated, may hold values from 0.099609375 to 1.8984375
- w_query: bfloat16 [2048, 2048], P('cp', 'tp'), may hold values from -0.125 to 0.125
- w_key: bfloat16 [2048, 2048], P('cp', 'tp'), may hold values from -0.125 to 0.125
- w_value: bfloat16 [2048, 2048], P('cp', 'tp'), may hold values from -0.125 to 0.125
- w_output: bfloat16 [2048, 2048], P('cp', 'tp'), may hold values from -2 to 2
- ffn_gain: bfloat16 [2048], P('cp'), may hold values from 0.099609375 to 1.8984375
- w_router: bfloat16 [2048, 8], P('cp'), may hold values from -0.25 to 0.25
- w_gate: bfloat16 [2048, 8, 1024], P('cp', None, 'tp'), may hold values from -0.125 to 0.125
- w_up: bfloat16 [2048, 8, 1024], P('cp', None, 'tp'), may hold values from -0.125 to 0.125
- w_down: bfloat16 [2048, 8, 1024], P('cp', None, 'tp'), may hold values from -0.75 to 0.75
- cotangent: bfloat16 [2048, 2048], P('cp'), may hold values from -6 to 6
Outputs:
- block_out: bfloat16 [2048, 2048], P('cp')
- grad_in: float32 [2048, 2048], P('cp')
- grad_attn_gain: float32 [2048], P('cp')
- grad_q_gain: float32 [128], replicated
- grad_k_gain: float32 [128], replicated
- grad_query: float32 [2048, 2048], P('cp', 'tp')
- grad_key: float32 [2048, 2048], P('cp', 'tp')
- grad_value: float32 [2048, 2048], P('cp', 'tp')
- grad_output: float32 [2048, 2048], P('cp', 'tp')
- grad_ffn_gain: float32 [2048], P('cp')
- grad_router: float32 [2048, 8], P('cp')
- grad_gate: float32 [2048, 8, 1024], P('cp', None, 'tp')
- grad_up: float32 [2048, 8, 1024], P('cp', None, 'tp')
- grad_down: float32 [2048, 8, 1024], P('cp', None, 'tp')
Inputs may be any that keep to these rules, and one draw needn't show every extreme that they name: `doc_ids`: document numbers never fall along the stream; every document holds 1 to 1024 tokens and one holds exactly 1024. `expert_ids`: the 2 experts of a token differ. Among the tokens of one index of cp no expert is named more than 96 times, and on some index some expert is named exactly 96 times.
All inputs are finite; a program needn't handle non-finite values.
Results may differ from a plain program's by a relative error of at most 0.025.
Values may be sent and summed in bfloat16 or wider, within the bound.
A program may use at most 256 MiB of HBM per device.

v0:
```python
import functools
import types

import jax
import jax.numpy as jnp
import numpy as np
from jax import lax
from jax.experimental import pallas as pl
from jax.experimental.pallas import tpu as pltpu
from jax.sharding import Mesh
from jax.sharding import PartitionSpec as P

eps = 1e-05
theta = 50000.0
negative = -1e30
AXES = ("b", "a", "y", "c")
MESH = pl.DeviceIdType.MESH
bf16 = jnp.bfloat16
f32 = jnp.float32


NT = (((1,), (1,)), ((), ()))
TN = (((0,), (0,)), ((), ()))


def dot(left, right, dims=(((1,), (0,)), ((), ()))):
    return lax.dot_general(left, right, dims, preferred_element_type=f32)


class Net:
    def __init__(self, sizes, send, recv):
        self.sizes, self.send, self.recv, self.used = sizes, send, recv, 0
        self.me = {axis: lax.axis_index(axis) for axis in AXES}

    def near(self, **offs):
        return {axis: lax.rem(self.me[axis] + off, self.sizes[axis]) for axis, off in offs.items()}

    def copy(self, source, target, place):
        slot = self.used
        self.used += 1
        return pltpu.make_async_remote_copy(
            src_ref=source,
            dst_ref=target,
            send_sem=self.send.at[slot],
            recv_sem=self.recv.at[slot],
            device_id=place,
            device_id_type=MESH,
        )

    def greet(self, places):
        barrier = pltpu.get_barrier_semaphore()
        for place in places:
            pl.semaphore_signal(barrier, inc=1, device_id=place, device_id_type=MESH)
        pl.semaphore_wait(barrier, len(places))

    def pick(self, *values):
        result = values[-1]
        for i in range(len(values) - 2, -1, -1):
            result = jnp.where(self.me["b"] == i, values[i], result)
        return result

    def reduce(self, *args):
        return Reduce(self, *args)

    def spread(self, *blocks, start=True):
        return Spread(self, blocks, start)


class Reduce:
    def __init__(self, net, parts, got, make=None):
        self.net, self.parts, self.got = net, parts, got
        self.b = b = net.me["b"]
        self.base = net.used
        net.used += 4
        self.order = [3 - b, net.pick(2, 0, 3, 1), net.pick(1, 3, 0, 2)]
        if make is None:
            for k in range(2):
                self.hop(self.order[k]).start()
            return
        if net.sizes["a"] > 2:
            for k in range(3):
                make(self.order[k])
                if k < 2:
                    self.hop(self.order[k]).start()
            return

        @pl.loop(0, 3)
        def _(k):
            d = jnp.where(k == 0, self.order[0], jnp.where(k == 1, self.order[1], self.order[2]))
            make(d)

            @pl.when(k < 2)
            def _():
                self.hop(d).start()

    def hop(self, d):
        net, b = self.net, self.b
        far = ((b == 0) & (d == 3)) | ((b == 3) & (d == 0))
        beside = jnp.where(b == 0, 1, 2)
        target, slot = jnp.where(far, beside, d), jnp.where(far, beside, b)
        return pltpu.make_async_remote_copy(
            src_ref=self.parts.at[d],
            dst_ref=self.got.at[slot],
            send_sem=net.send.at[self.base + d],
            recv_sem=net.recv.at[self.base + slot],
            device_id={"b": target},
            device_id_type=MESH,
        )

    def came(self, i):
        net = self.net
        return pltpu.make_async_remote_copy(
            src_ref=self.got.at[i],
            dst_ref=self.got.at[i],
            send_sem=net.send.at[self.base + i],
            recv_sem=net.recv.at[self.base + i],
            device_id=net.near(b=1),
            device_id_type=MESH,
        )

    def inner(self):
        b, d = self.b, self.order[2]

        @pl.when((b == 1) | (b == 2))
        def _():
            self.came(b).wait_recv()
            rows = self.parts.shape[1]
            step = 256 if rows % 256 == 0 else rows

            @pl.loop(0, rows // step)
            def _(i):
                sl = pl.ds(pl.multiple_of(i * step, step), step)
                total = self.parts[d, sl, :].astype(f32) + self.got[b, sl, :].astype(f32)
                self.parts[d, sl, :] = total.astype(bf16)

        self.hop(d).start()

    def wait(self):
        for i in range(4):

            @pl.when((self.b != i) & (jnp.abs(self.b - i) <= 2))
            def _():
                self.came(i).wait_recv()

    def total(self, *index):
        b = self.b
        value = self.parts[(b,) + index].astype(f32)
        for i in range(4):
            valid = (b != i) & (jnp.abs(b - i) <= 2)
            value = value + jnp.where(valid, self.got[(i,) + index].astype(f32), 0.0)
        return value

    def finish(self):
        for d in range(4):

            @pl.when(self.b != d)
            def _():
                self.hop(d).wait_send()


class Spread:
    def __init__(self, net, blocks, start):
        self.net, self.blocks = net, blocks
        self.b = b = net.me["b"]
        self.base = net.used
        net.used += 4 * len(blocks)
        self.targets = [net.pick(2, 3, 0, 1), net.pick(1, 0, 3, 2), net.pick(2, 2, 1, 1)]
        self.order = [net.pick(1, 3, 0, 2), net.pick(2, 0, 3, 1), net.pick(3, 2, 1, 0)]
        self.inner = (b == 1) | (b == 2)
        if start:
            self.begin()

    def begin(self):
        for k, target in enumerate(self.targets):
            if k < 2:
                for j in range(len(self.blocks)):
                    self.hop(self.b, target, target, j).start()
            else:

                @pl.when(self.inner)
                def _():
                    for j in range(len(self.blocks)):
                        self.hop(self.b, target, target, j).start()

    def hop(self, i, target, slot, j):
        net, count = self.net, len(self.blocks)
        return pltpu.make_async_remote_copy(
            src_ref=self.blocks[j](i),
            dst_ref=self.blocks[j](i),
            send_sem=net.send.at[self.base + slot * count + j],
            recv_sem=net.recv.at[self.base + i * count + j],
            device_id={"b": target},
            device_id_type=MESH,
        )

    def take(self, i):
        b = self.b
        onward = ((b == 1) & (i == 3)) | ((b == 2) & (i == 0))
        for j in range(len(self.blocks)):
            self.hop(i, self.net.near(b=1)["b"], b, j).wait_recv()

            @pl.when(onward)
            def _():
                self.hop(i, jnp.where(b == 1, 0, 3), b, j).start()

    def take_all(self):
        for i in self.order:
            self.take(i)

    def finish(self):
        b = self.b
        for k, target in enumerate(self.targets):
            for j in range(len(self.blocks)):
                if k < 2:
                    self.hop(b, target, target, j).wait_send()
                else:

                    @pl.when(self.inner)
                    def _():
                        self.hop(b, target, target, j).wait_send()
                        self.hop(b, jnp.where(b == 1, 0, 3), b, j).wait_send()


def rope(values, cos_tab, sin_tab):
    return values * cos_tab + pltpu.roll(values, values.shape[1] // 2, 1) * sin_tab


def head_norm(values):
    return lax.rsqrt(jnp.mean(values * values, axis=1, keepdims=True) + eps)


def unrope(grad, raw, gain, cos_tab, sin_tab):
    factor = head_norm(raw)
    normed = raw * factor
    turned = grad * cos_tab + pltpu.roll(grad * sin_tab, grad.shape[1] // 2, 1)
    gain_part = jnp.sum(turned * normed, axis=0, keepdims=True)
    inner = turned * gain
    slope = jnp.mean(raw * inner, axis=1, keepdims=True)
    return factor * inner - raw * (factor * factor * factor * slope), gain_part


class TwoLevel:
    def __init__(self, net, acc, sendc, recvc, sendy, recvy, kinds):
        self.net, self.acc = net, acc
        self.sendc, self.recvc, self.sendy, self.recvy = sendc, recvc, sendy, recvy
        self.base = net.used
        self.kinds = kinds
        net.used += 8 * kinds
        self.part = acc.shape[2]
        self.half = acc.shape[1]

    def lane(self, j):
        return slice(j * self.part, (j + 1) * self.part)

    def hop(self, i, j, level):
        net = self.net
        source, target = ((self.sendc, self.recvc), (self.sendy, self.recvy))[level]
        slot = self.base + 4 * self.kinds * level + self.kinds * i + j
        lane = pl.ds(j * self.part, self.part)
        return pltpu.make_async_remote_copy(
            src_ref=source.at[i, :, lane],
            dst_ref=target.at[i, :, lane],
            send_sem=net.send.at[slot],
            recv_sem=net.recv.at[slot],
            device_id=net.near(c=1) if level == 0 else net.near(y=1),
            device_id_type=MESH,
        )

    def put(self, i, j, term, k):
        first = self.net.me["c"] == 0
        low, high = term[: self.half], term[self.half :]
        self.acc[k] = jnp.where(first, low, high)
        self.sendc[i, :, self.lane(j)] = jnp.where(first, high, low).astype(bf16)
        self.hop(i, j, 0).start()

    def onward(self, i, j, k):
        self.hop(i, j, 0).wait_recv()
        total = self.acc[k] + self.recvc[i, :, self.lane(j)].astype(f32)
        self.sendy[i, :, self.lane(j)] = total.astype(bf16)
        self.hop(i, j, 1).start()

    def total(self, i, j):
        self.hop(i, j, 1).wait_recv()
        lane = self.lane(j)
        return self.sendy[i, :, lane].astype(f32) + self.recvy[i, :, lane].astype(f32)

    def finish(self, kinds=(0,)):
        for i in range(4):
            for j in kinds:
                self.hop(i, j, 0).wait_send()
                self.hop(i, j, 1).wait_send()


def transpose_columns(columns, rows):
    lane = lax.broadcasted_iota(jnp.int32, (rows, 128), 1)
    table = jnp.zeros((rows, 128), f32)
    for k, column in enumerate(columns):
        table = jnp.where(lane == k, column, table)
    return jnp.transpose(table)[:8, :]


INS = (
    "tok", "cot", "wq_in", "wk_in", "wv_in", "wo_in", "wg_in", "wu_in", "wd_in", "ids_in",
    "docs_in", "router_in", "gain_in_a", "gain_in_f", "gain_q", "gain_k", "speed_in",
)
OUTS = (
    "out_rows", "in_rows", "gate_own", "up_own", "down_own", "gate_in", "up_in", "down_in",
    "proj_out", "tail",
)
WORK = (
    "xc", "cotc", "rows_all", "rows_own", "cols_own", "cols_all", "cols_sum", "wqkv", "wo",
    "wg", "wu", "wd", "stage", "hn", "raw", "q_rot", "kv", "stat", "ho", "cos_tab", "sin_tab",
    "pkv", "gkv", "pq", "gq", "pcd", "gcd", "acc", "sendc", "recvc", "sendy", "recvy", "hidden", "d_hidden", "scaled",
    "small", "small_in", "pay", "wide", "pair", "late_small", "extra_own", "extra_in", "d_attn",
    "out_half", "block_out", "head_acc", "dkv_acc", "dkv_send", "dkv_in", "gsend", "gin_w",
    "gout", "gout_in", "gin", "s4", "gain_acc", "tail_all", "gains", "ids", "docs", "proj",
    "send", "recv", "local",
)


def layer_kernel(sizes, dims, *refs):
    r = types.SimpleNamespace(**dict(zip(INS + OUTS + WORK, refs)))
    nb, na, head, heads, experts, ff, top = dims
    net = Net(sizes, r.send, r.recv)
    me = net.me
    b, a, y, c = me["b"], me["a"], me["y"], me["c"]
    tok, part = r.xc.shape[1], r.xc.shape[2]
    half, col, model, width, sub = tok // 2, nb * tok, nb * part, heads * head, part // na
    scale = head**-0.5
    mine = pl.ds(pl.multiple_of(c * half, half), half)
    own_lane = pl.ds(pl.multiple_of(b * part, part), part)
    head_lane = pl.ds(pl.multiple_of(b * head, head), head)
    core, across = net.near(c=1), net.near(y=1)
    b_peers = [net.near(b=k) for k in range(1, nb)]
    a_peers = [net.near(a=k) for k in range(1, na)]
    group = [
        net.near(b=i, y=j, c=k)
        for i in range(nb) for j in range(2) for k in range(2) if i or j or k
    ]
    tp_peers = [net.near(y=j, c=k) for j in range(2) for k in range(2) if j or k]
    sent = []
    local_used = [0]

    def rows_of(i):
        return pl.ds(pl.multiple_of(i * tok, tok), tok)

    def lane_of(place):
        return pl.ds(pl.multiple_of(place * part, part), part)

    def move(source, target):
        copy = pltpu.make_async_copy(source, target, r.local.at[local_used[0]])
        local_used[0] += 1
        copy.start()
        return copy

    def ship(source, target, place):
        copy = net.copy(source, target, place)
        copy.start()
        sent.append(copy)
        return copy

    def arrive(copies):
        for copy in copies:
            copy.wait_recv()

    def drain(copies):
        for copy in copies:
            copy.wait_send()
            sent[:] = [other for other in sent if other is not copy]

    tok_here = move(r.tok, r.gin)
    w_here = [move(w, r.wqkv.at[j, a]) for j, w in ((1, r.wk_in), (2, r.wv_in), (0, r.wq_in))]
    stage_copy = move(r.wd_in, r.stage)
    late_here = [move(r.wo_in, r.wo.at[a]), move(r.cot.at[:, own_lane], r.cotc.at[b])]
    net.greet(group + [net.near(b=j, a=k) for j in range(nb) for k in range(1, na)])

    r.cols_own[...] = jnp.zeros_like(r.cols_own)
    r.cols_own[0:experts, :] = r.router_in[...].astype(f32)
    r.cols_own[experts : experts + 1, :] = r.gain_in_a[...].astype(f32).reshape(1, sub)
    r.cols_own[experts + 1 : experts + 2, :] = r.gain_in_f[...].astype(f32).reshape(1, sub)
    r.gains[0:1, :] = r.gain_q[...].astype(f32)
    r.gains[1:2, :] = r.gain_k[...].astype(f32)
    r.gains[2:3, :] = r.speed_in[...]
    r.rows_own[...] = jnp.zeros_like(r.rows_own)
    r.rows_own[1 : 1 + top, :] = r.ids_in[...].astype(f32)
    r.rows_own[3:4, :] = r.docs_in[...].astype(f32)

    exchange = [net.pick(2, 3, 0, 1), net.pick(3, 2, 1, 0), net.pick(1, 0, 3, 2)]

    quarter = half // 2
    fourth = pl.ds(pl.multiple_of(c * half + y * quarter, quarter), quarter)

    def to_quarters(source, target):
        return [
            ship(source.at[fourth, lane_of(d)], target.at[b, fourth, :], {"b": d})
            for d in exchange
        ]

    def over_a(source, target):
        return [ship(source, target.at[a], place) for place in a_peers]

    def onward(copies, target, rows, place):
        more = []
        for source_b, copy in zip(exchange, copies):
            copy.wait_recv()
            block = target.at[source_b, rows, :]
            more.append(ship(block, block, place))
        return more

    x_copies = to_quarters(r.tok, r.xc)
    cols_copies = over_a(r.cols_own, r.cols_all)
    r.cols_all[a] = r.cols_own[...]
    kv_weights = over_a(r.wk_in, r.wqkv.at[1]) + over_a(r.wv_in, r.wqkv.at[2])
    q_weights = over_a(r.wq_in, r.wqkv.at[0])
    tok_here.wait()
    square_columns = []
    for s in range(tok // 64):
        piece = r.gin[s * 64 : (s + 1) * 64, :].astype(f32)
        square_columns.append(jnp.sum(piece * piece, axis=1, keepdims=True))
    squares = transpose_columns([jnp.concatenate(square_columns, axis=0)], tok)[0:1, :]
    which8 = lax.broadcasted_iota(jnp.int32, (8, tok), 0)
    r.rows_own[0:1, :] = lax.rsqrt(squares / model + eps)
    rows_copies = [ship(r.rows_own, r.rows_all.at[a, b], place) for place in b_peers]
    rows_far = [
        ship(r.rows_own, r.rows_all.at[a, b], net.near(b=j, a=k))
        for j in range(nb) for k in range(1, na)
    ]
    r.rows_all[a, b] = r.rows_own[...]
    r.xc[b] = r.gin[:, own_lane]
    cot_copies = to_quarters(r.cot, r.cotc)
    wo_copies = over_a(r.wo_in, r.wo)

    def relayout(target):
        step = 32

        @pl.loop(0, sub // step)
        def _(n):
            rows = pl.ds(pl.multiple_of(n * step, step), step)
            turned = jnp.swapaxes(r.stage[rows].astype(f32), 0, 1)
            for e in range(experts):
                target[a, rows, e * ff : (e + 1) * ff] = turned[e].astype(bf16)

    stage_copy.wait()
    relayout(r.wd)
    wd_copies = over_a(r.wd.at[a], r.wd)
    stage_copy = move(r.wg_in, r.stage)

    lane_index = lax.broadcasted_iota(jnp.int32, (tok, head), 1)
    row_index = lax.broadcasted_iota(jnp.int32, (tok, head), 0)

    @pl.loop(0, nb)
    def _(i):
        place = ((i * na + a) * tok + row_index).astype(f32)
        angle = place * r.gains[2:3, :]
        r.cos_tab[rows_of(i), :] = jnp.cos(angle)
        turned = jnp.sin(angle)
        r.sin_tab[rows_of(i), :] = jnp.where(lane_index < head // 2, -turned, turned)

    x_y = onward(x_copies, r.xc, fourth, across)
    x_more = onward(x_y, r.xc, mine, core)
    arrive(rows_copies + cols_copies + x_more)
    arrive(kv_weights)
    for copy in w_here:
        copy.wait()
    for k in range(na):
        r.cols_sum[:, k * sub : (k + 1) * sub] = r.cols_all[k]
    gain_in = r.cols_sum[experts : experts + 1, :]
    for i in range(nb):
        columns = jnp.transpose(r.rows_all[a, i])
        r.ids[i] = columns
        r.hn[i] = (r.xc[i].astype(f32) * columns[:, 0:1] * gain_in).astype(bf16)

    def weight(j):
        return r.wqkv[j].reshape(part, width)

    @pl.loop(0, nb)
    def _(i):
        for j in (1, 2):
            term = dot(r.hn[i], weight(j)).astype(bf16)
            for h in range(heads):
                piece = term[:, h * head : (h + 1) * head]
                r.pkv[h, rows_of(i), (j - 1) * head : j * head] = piece

    kv_sum = net.reduce(r.pkv, r.gkv)
    cot_y = onward(cot_copies, r.cotc, fourth, across)
    arrive(q_weights)

    @pl.loop(0, nb)
    def _(i):
        term = dot(r.hn[i], weight(0)).astype(bf16)
        for h in range(heads):
            r.pq[h, rows_of(i), :] = term[:, h * head : (h + 1) * head]

    stage_copy.wait()
    relayout(r.wg)
    low, high = (pl.ds(k * experts * ff // 2, experts * ff // 2) for k in range(2))

    def half_over_a(array, lane):
        return [ship(array.at[a, :, lane], array.at[a, :, lane], place) for place in a_peers]

    wg_copies = half_over_a(r.wg, low)
    stage_copy = move(r.wu_in, r.stage)
    kv_sum.inner()
    q_sum = net.reduce(r.pq, r.gq)
    stage_copy.wait()
    relayout(r.wu)
    q_sum.inner()
    cot_more = onward(cot_y, r.cotc, mine, core)
    kv_sum.wait()

    @pl.loop(0, nb)
    def _(i):
        rows = rows_of(i)
        both = kv_sum.total(rows)
        r.raw[rows, head:] = both
        keys = both[:, :head]
        normed = keys * head_norm(keys) * r.gains[1:2, :]
        r.kv[a, rows, :head] = rope(normed, r.cos_tab[rows, :], r.sin_tab[rows, :]).astype(bf16)
        r.kv[a, rows, head:] = both[:, head:].astype(bf16)

    kv_copies = over_a(r.kv.at[a], r.kv)
    wg_copies += half_over_a(r.wg, high)
    wu_copies = over_a(r.wu.at[a], r.wu)
    arrive(wd_copies + cot_more)
    for copy in late_here:
        copy.wait()

    def chosen(left, weights, d, put):
        columns = r.ids[d]
        values = [jnp.zeros((tok, ff), f32) for k in range(top)]
        for e in range(experts):
            term = dot(left, weights[:, :, e * ff : (e + 1) * ff].reshape(part, ff))
            for k in range(top):
                values[k] = jnp.where(columns[:, 1 + k : 2 + k] == e, term, values[k])
        for k in range(top):
            put(k, values[k].astype(bf16))

    groups = ff // head

    @pl.loop(0, nb)
    def _(i):
        def put(k, value):
            for g in range(groups):
                r.pcd[k, i, g * tok : (g + 1) * tok, :] = value[:, g * head : (g + 1) * head]

        chosen(r.cotc[i], r.wd, i, put)

    cd_sums = [net.reduce(r.pcd.at[0], r.gcd.at[0])]
    arrive(rows_far)
    for i in range(nb):
        for j in range(na):
            r.docs[j, :, i * tok : (i + 1) * tok] = r.rows_all[j, i][3:4, :]
    q_sum.wait()

    @pl.loop(0, nb)
    def _(i):
        rows = rows_of(i)
        query = q_sum.total(rows)
        r.raw[rows, :head] = query
        normed = query * head_norm(query) * r.gains[0:1, :]
        r.q_rot[rows, :] = rope(normed, r.cos_tab[rows, :], r.sin_tab[rows, :]).astype(bf16)

    cd_sums[0].inner()

    deep = 2 if na <= 2 else 1

    def deep_rows(i):
        return pl.ds(pl.multiple_of(i * deep * tok, deep * tok), deep * tok)

    def deep_ids(i):
        return r.ids[pl.ds(i * deep, deep)].reshape(deep * tok, 8)

    def attend(block, first, last):
        @pl.loop(0, nb)
        def _(i):
            rows = rows_of(i)
            columns = r.ids[i]
            scores = dot(r.q_rot[rows, :], r.kv[block, :, :head], NT) * scale
            scores = jnp.where(columns[:, 3:4] == r.docs[block], scores, negative)
            most = jnp.max(scores, axis=1, keepdims=True)
            if not first:
                before = r.stat[rows, 0:1]
                most = jnp.maximum(before, most)
            terms = jnp.exp(scores - most)
            total = jnp.sum(terms, axis=1, keepdims=True)
            mixed = dot(terms.astype(bf16), r.kv[block, :, head:])
            if not first:
                fade = jnp.exp(before - most)
                total = r.stat[rows, 1:2] * fade + total
                mixed = r.head_acc[rows, :] * fade + mixed
            if last:
                r.ho[rows, head_lane] = (mixed * (1.0 / total)).astype(bf16)
                r.stat[rows, 2:3] = most + jnp.log(total)
            else:
                r.stat[rows, 0:1] = most
                r.stat[rows, 1:2] = total
                r.head_acc[rows, :] = mixed

    attend(a, True, na == 1)
    for k in range(1, na):
        kv_copies[k - 1].wait_recv()
        attend(lax.rem(a + na - k, na), False, k == na - 1)

    def head_block(array, i, start, size):
        return array.at[pl.ds(start, size), pl.ds(pl.multiple_of(i * head, head), head)]

    def chain(lines, i):
        lines[i].take(lines[i].order[0])
        if i + 2 < len(lines):
            lines[i + 2].begin()

    def rest(line):
        line.take(line.order[1])
        line.take(line.order[2])

    ho_lines = [
        net.spread(lambda i, s=s: head_block(r.ho, i, s * tok, tok), start=s < 2)
        for s in range(nb)
    ]
    arrive(wo_copies)

    mixer = TwoLevel(net, r.acc, r.sendc, r.recvc, r.sendy, r.recvy, 1)
    for i in range(nb):
        chain(ho_lines, i)
        rest(ho_lines[i])
        if i == nb - 1:
            for k in range(1, top):
                cd_sums.append(net.reduce(r.pcd.at[k], r.gcd.at[k]))
        term = dot(r.ho[i * tok : (i + 1) * tok, :], r.wo[...].reshape(part, width), NT)
        mixer.put(i, 0, term, i)
        if i:
            mixer.onward(i - 1, 0, i - 1)
    mixer.onward(nb - 1, 0, nb - 1)
    for group_sum in cd_sums[1:]:
        group_sum.inner()
    gain_mid = r.cols_sum[experts + 1 : experts + 2, :]
    router = r.cols_sum[...].astype(bf16)
    last_copies = []
    for i in range(nb):
        value = r.xc[i, mine, :].astype(f32) + mixer.total(i, 0)
        r.hidden[i] = value
        piece = (value * gain_mid).astype(bf16)
        r.scaled[i, mine, :] = piece
        logits = dot(router, piece, NT)
        squares = jnp.sum(value * value, axis=1, keepdims=True)
        squares = jnp.transpose(jnp.broadcast_to(squares, (half, 128)))[:1, :]
        which = lax.broadcasted_iota(jnp.int32, logits.shape, 0)
        r.small[i, :, mine] = jnp.where(which == experts, squares, logits)
        for array in (r.scaled.at[i, mine, :], r.small.at[i, :, mine]):
            last_copies.append(ship(array, array, core))
    arrive(wg_copies + wu_copies + last_copies)
    mixer.finish()
    kv_sum.finish()
    q_sum.finish()

    small_copies = [ship(r.small.at[p["b"]], r.small_in.at[b], p) for p in b_peers]
    r.small_in[b] = r.small[b]

    def make(d):
        for j, w in enumerate((r.wg, r.wu)):

            def put(k, value, j=j):
                r.pkv[d, (2 * k + j) * tok : (2 * k + j + 1) * tok, :] = value

            chosen(r.scaled[d], w, d, put)

    gu_sum = net.reduce(r.pkv, r.gkv, make)
    gu_sum.inner()
    make(b)
    arrive(small_copies)
    for group_sum in cd_sums:
        group_sum.wait()
    gu_sum.wait()
    total = jnp.sum(r.small_in[...], axis=0)
    r_mid = lax.rsqrt(total[experts : experts + 1] / model + eps)
    logits = total[:experts] * r_mid
    terms = jnp.exp(logits - jnp.max(logits, axis=0, keepdims=True))
    probs = terms / jnp.sum(terms, axis=0, keepdims=True)
    which = lax.broadcasted_iota(jnp.int32, probs.shape, 0).astype(f32)
    picks = [r.rows_own[1 + k : 2 + k] == which for k in range(top)]
    combine = [jnp.sum(jnp.where(pick, probs, 0.0), axis=0, keepdims=True) for pick in picks]
    table = jnp.where(which8 == 0, r_mid, 0.0)
    for k in range(top):
        table = jnp.where(which8 == 1 + k, combine[k], table)
    columns = jnp.transpose(table)
    r_col = columns[:, 0:1]
    columns_back = []
    inner = jnp.zeros((tok, 1), f32)
    for k in range(top):
        gate = gu_sum.total(slice((2 * k) * tok, (2 * k + 1) * tok)) * r_col
        up = gu_sum.total(slice((2 * k + 1) * tok, (2 * k + 2) * tok)) * r_col
        back = jnp.concatenate(
            [
                cd_sums[k].total(slice(g * tok, (g + 1) * tok))
                for g in range(groups)
            ],
            axis=1,
        )
        sig = 1.0 / (1.0 + jnp.exp(-gate))
        silu = gate * sig
        act = silu * up
        weighed = columns[:, 1 + k : 2 + k]
        d_act = weighed * back
        d_gate = d_act * up * (sig * (1.0 + gate * (1.0 - sig)))
        d_up = d_act * silu
        for j, value in enumerate((weighed * act, d_gate * r_col, d_up * r_col)):
            r.pay[b, :, (top * j + k) * ff : (top * j + k + 1) * ff] = value.astype(bf16)
        columns_back.append(jnp.sum(act * back, axis=1, keepdims=True))
        inner = inner + jnp.sum(d_gate * gate + d_up * up, axis=1, keepdims=True)

    pay_line = net.spread(lambda i: r.pay.at[i, :, pl.ds(top * ff, 2 * top * ff)])
    act_lines = [
        net.spread(lambda i, k=k: r.pay.at[i, :, pl.ds(k * ff, ff)], start=False)
        for k in range(top)
    ]
    rank = y * sizes["c"] + c
    r.pair[rank] = transpose_columns(columns_back + [inner], tok)
    arrive([ship(r.pair.at[rank], r.pair.at[rank], place) for place in tp_peers])
    sums = r.pair[0] + r.pair[1] + r.pair[2] + r.pair[3]
    d_probs = jnp.zeros_like(probs)
    for k in range(top):
        d_probs = d_probs + jnp.where(picks[k], sums[k : k + 1], 0.0)
    d_logits = probs * (d_probs - jnp.sum(probs * d_probs, axis=0, keepdims=True))
    inner_row = sums[top : top + 1] + jnp.sum(d_logits * logits, axis=0, keepdims=True)
    r.late_small[b, 0:8, :] = d_logits * r_mid
    r.late_small[b, 8:16, :] = jnp.broadcast_to(r_mid * r_mid * inner_row / model, (8, tok))
    late_copies = [ship(r.late_small.at[b], r.late_small.at[b], place) for place in b_peers]

    mixer = TwoLevel(net, r.acc, r.sendc, r.recvc, r.sendy, r.recvy, 2)
    pieces = experts * ff // width
    by_piece = width // ff

    def expand(j, i, e):
        columns = r.ids[i]
        value = jnp.zeros((tok, ff), f32)
        for k in range(top):
            taken = r.pay[i, :, (top * j + k) * ff : (top * j + k + 1) * ff].astype(f32)
            value = jnp.where(columns[:, 1 + k : 2 + k] == e, taken, value)
        return value.astype(bf16)

    def use(i):
        def widen(j):
            for e in range(experts):
                g, h = e // by_piece, e % by_piece
                r.wide[j, g * tok : (g + 1) * tok, h * ff : (h + 1) * ff] = expand(j, i, e)

        def times(j, w):
            total = 0.0
            for g in range(pieces):
                piece = w[:, :, g * width : (g + 1) * width].reshape(part, width)
                total = total + dot(r.wide[j, g * tok : (g + 1) * tok, :], piece, NT)
            return total

        widen(1)
        widen(2)
        mixer.put(i, 0, times(1, r.wg) + times(2, r.wu), 0)
        mixer.onward(i, 0, 0)

    @pl.loop(0, nb)
    def _(n):
        index = b
        for k in range(nb - 1):
            index = jnp.where(n == k + 1, pay_line.order[k], index)

        @pl.when(n > 0)
        def _():
            pay_line.take(index)

        @pl.when(n == jnp.where(pay_line.inner, 1, 3))
        def _():
            act_lines[0].begin()

        use(index)

    drain(wd_copies + wg_copies + wu_copies)
    gu_sum.finish()

    def to_a(source, target):
        return [ship(source.at[p["a"]], target.at[k], p) for k, p in enumerate(a_peers)]

    def expert_grad(j, left, target, part_of):
        @pl.loop(part_of * experts // 2, (part_of + 1) * experts // 2)
        def _(e):
            for i in range(nb):
                r.pkv[0, i * tok : (i + 1) * tok, :] = expand(j, i, e)
            grad = dot(left[...].reshape(col, part), r.pkv[0], TN).astype(bf16)
            lane = pl.ds(pl.multiple_of(e * ff, ff), ff)
            for k in range(na):
                target[k, :, lane] = grad[k * sub : (k + 1) * sub, :]

    def half_to_a(source, target, part_of):
        lane = (low, high)[part_of]
        return [
            ship(source.at[p["a"], :, lane], target.at[k, :, lane], p)
            for k, p in enumerate(a_peers)
        ]

    expert_grad(1, r.scaled, r.wg, 0)
    pending = half_to_a(r.wg, r.gate_in, 0)
    arrive(late_copies)
    which16 = lax.broadcasted_iota(jnp.int32, (16, tok), 0)
    ffn_part = jnp.zeros((1, part), f32)
    attn_copies = []
    for i in range(nb):
        columns = jnp.transpose(r.late_small[i, :, mine])
        d_log = jnp.where(which16[:, :half] < experts, r.late_small[i, :, mine], 0.0).astype(bf16)
        mid = mixer.total(i, 0) + dot(d_log, router, TN)
        value = r.hidden[i]
        grad = r.cotc[i, mine, :].astype(f32) + gain_mid * mid - value * columns[:, 8:9]
        r.d_attn[i, mine, :] = grad.astype(bf16)
        attn_copies.append(ship(r.d_attn.at[i, mine, :], r.d_attn.at[i, mine, :], core))
        ffn_part = ffn_part + jnp.sum(mid * value, axis=0, keepdims=True)
        r.d_hidden[i] = grad
    act_lines[0].take(act_lines[0].order[0])
    arrive(attn_copies)

    @pl.loop(0, nb)
    def _(i):
        term = dot(r.d_attn[i], r.wo[...].reshape(part, width)).astype(bf16)
        for h in range(heads):
            r.pq[h, rows_of(i), :] = term[:, h * head : (h + 1) * head]

    heads_sum = net.reduce(r.pq, r.gq)

    expert_grad(1, r.scaled, r.wg, 1)
    pending += half_to_a(r.wg, r.gate_in, 1)
    results = [move(r.wg.at[a], r.gate_own)]
    heads_sum.inner()
    expert_grad(2, r.scaled, r.wu, 0)

    def experts_out():
        for line in act_lines:
            rest(line)

        @pl.loop(0, nb)
        def _(i):
            total = 0.0
            for e in range(experts):
                r.pkv[1, 0:tok, :] = expand(0, i, e)
                piece = r.wd[:, :, e * ff : (e + 1) * ff].reshape(part, ff)
                total = total + dot(r.pkv[1, 0:tok, :], piece, NT)
            mixer.put(i, 1, total, i)

    term = dot(r.d_attn[...].reshape(col, part), r.ho[...], TN).astype(bf16)
    r.gout[...] = term.reshape(na, sub, width)
    pending += to_a(r.gout, r.gout_in)
    extra = 0.0
    for i in range(nb):
        d_log = jnp.where(which16 < experts, r.late_small[i], 0.0).astype(bf16)
        extra = extra + dot(d_log, r.scaled[i])
    which_row = lax.broadcasted_iota(jnp.int32, (16, part), 0)
    r.extra_own[...] = jnp.where(which_row == experts + 1, ffn_part, extra)
    heads_sum.wait()
    for line in act_lines[1:]:
        line.begin()

    r.gain_acc[...] = jnp.zeros_like(r.gain_acc)

    @pl.loop(0, nb)
    def _(i):
        rows = rows_of(i)
        cot = heads_sum.total(rows).astype(bf16)
        r.pq[b, rows, :] = cot
        delta = jnp.sum(cot.astype(f32) * r.ho[rows, head_lane].astype(f32), axis=1, keepdims=True)
        r.stat[rows, 4:5] = delta

    def attend_back(block, first, last, start, stop):
        @pl.loop(start // deep, stop // deep)
        def _(i):
            rows = deep_rows(i)
            columns = deep_ids(i)
            query, cot = r.q_rot[rows, :], r.pq[b, rows, :]
            keys, values = r.kv[block, :, :head], r.kv[block, :, head:]
            scores = dot(query, keys, NT) * scale
            keep = columns[:, 3:4] == r.docs[block]
            probs = jnp.where(keep, jnp.exp(scores - r.stat[rows, 2:3]), 0.0)
            d_scores = (probs * (dot(cot, values, NT) - r.stat[rows, 4:5])).astype(bf16)
            key_term = dot(d_scores, query, TN) * scale
            value_term = dot(probs.astype(bf16), cot, TN)

            @pl.when(i == 0)
            def _():
                r.dkv_acc[:, :head] = key_term
                r.dkv_acc[:, head:] = value_term

            @pl.when(i > 0)
            def _():
                r.dkv_acc[:, :head] += key_term
                r.dkv_acc[:, head:] += value_term

            grad = dot(d_scores, keys) * scale
            if not first:
                grad = r.head_acc[rows, :] + grad
            if not last:
                r.head_acc[rows, :] = grad
            else:
                source = r.raw[rows, :head]
                grad, gain_part = unrope(
                    grad, source, r.gains[0:1, :], r.cos_tab[rows, :], r.sin_tab[rows, :]
                )
                r.gain_acc[0:1, :] += gain_part
                r.wide[0, rows, head_lane] = grad.astype(bf16)
                r.stat[rows, 3:4] = jnp.sum(grad * source, axis=1, keepdims=True)

    kv_back = []
    for k in range(1, na):
        attend_back(lax.rem(a + k, na), k == 1, False, 0, nb)
        r.dkv_send[k - 1] = r.dkv_acc[...].astype(bf16)
        kv_back.append(ship(r.dkv_send.at[k - 1], r.dkv_in.at[k - 1], a_peers[k - 1]))
    for line in act_lines[1:]:
        line.take(line.order[0])
    pending += half_to_a(r.wu, r.up_in, 0)
    q_lines = []
    for s in range(2):
        attend_back(a, na == 1, True, s * (nb // 2), (s + 1) * (nb // 2))
        q_lines.append(
            net.spread(lambda i, s=s: head_block(r.wide.at[0], i, s * (col // 2), col // 2))
        )
    expert_grad(2, r.scaled, r.wu, 1)
    pending += half_to_a(r.wu, r.up_in, 1)
    results.append(move(r.wu.at[a], r.up_own))
    for line in q_lines:
        line.take(line.order[0])
    arrive(kv_back)

    @pl.loop(0, nb)
    def _(i):
        rows = rows_of(i)
        both = r.dkv_acc[rows, :]
        for k in range(na - 1):
            both = both + r.dkv_in[k, rows, :].astype(f32)
        source = r.raw[rows, head : 2 * head]
        grad, gain_part = unrope(
            both[:, :head], source, r.gains[1:2, :], r.cos_tab[rows, :], r.sin_tab[rows, :]
        )
        r.gain_acc[1:2, :] += gain_part
        value_grad = both[:, head:]
        r.wide[1, rows, head_lane] = grad.astype(bf16)
        r.wide[2, rows, head_lane] = value_grad.astype(bf16)
        r.stat[rows, 3:4] += jnp.sum(
            grad * source + value_grad * r.raw[rows, 2 * head :], axis=1, keepdims=True
        )

    place16 = (b * 2 + y) * 2 + c
    r.s4[place16] = transpose_columns([r.stat[i * tok : (i + 1) * tok, 3:4] for i in range(nb)], tok)
    r.s4[place16, 4:6, 0:head] = r.gain_acc[0:2, :]
    s4_copies = [ship(r.s4.at[place16], r.s4.at[place16], place) for place in group]

    def kv_piece(s):
        return net.spread(
            lambda i: head_block(r.wide.at[1], i, s * tok, tok),
            lambda i: head_block(r.wide.at[2], i, s * tok, tok),
            start=s < 2,
        )

    kv_lines = [kv_piece(s) for s in range(nb)]
    def weight_grad(j):
        grad = dot(r.hn[...].reshape(col, part), r.wide[j], TN).astype(bf16)
        r.gsend[j] = grad.reshape(na, sub, width)
        return to_a(r.gsend.at[j], r.gin_w.at[j])

    for line in q_lines:
        line.take(line.order[1])
        line.take(line.order[2])
    pending += weight_grad(0)
    mixer_in = TwoLevel(net, r.acc, r.sendc, r.recvc, r.sendy, r.recvy, 1)
    mixer.finish()
    def in_term(i):
        rest(kv_lines[i])
        rows = slice(i * tok, (i + 1) * tok)
        term = dot(r.wide[0, rows, :], weight(0), NT) + dot(r.wide[1, rows, :], weight(1), NT)
        mixer_in.put(i, 0, term + dot(r.wide[2, rows, :], weight(2), NT), i)
        mixer_in.onward(i, 0, i)

    chain(kv_lines, 0)
    experts_out()
    chain(kv_lines, 1)
    for i in range(nb):
        mixer.onward(i, 1, i)
    expert_grad(0, r.cotc, r.wd, 0)
    pending += half_to_a(r.wd, r.down_in, 0)
    arrive(s4_copies)
    in_term(0)
    chain(kv_lines, 2)
    expert_grad(0, r.cotc, r.wd, 1)
    pending += half_to_a(r.wd, r.down_in, 1)
    results.append(move(r.wd.at[a], r.down_own))
    in_term(1)
    chain(kv_lines, 3)
    for j in range(nb):
        r.out_half[j] = (r.hidden[j] + mixer.total(j, 1)).astype(bf16)
    r.block_out[mine, own_lane] = r.out_half[b]
    in_term(2)
    in_term(3)
    out_rows = pl.ds(pl.multiple_of(y * quarter, quarter), quarter)
    out_copies = [
        ship(r.out_half.at[d, out_rows, :], r.block_out.at[fourth, own_lane], {"b": d})
        for d in exchange
    ]

    def lanes_onward(copies, rows, place):
        more = []
        for source_b, copy in zip(exchange, copies):
            copy.wait_recv()
            block = r.block_out.at[rows, lane_of(source_b)]
            more.append(ship(block, block, place))
        return more

    pending += weight_grad(1)
    pending += weight_grad(2)
    sums = r.s4[0]
    for k in range(1, 4 * nb):
        sums = sums + r.s4[k]
    inner_columns = jnp.transpose(sums)
    attn_part = jnp.zeros((1, part), f32)
    in_hops = []
    base_in = net.used
    net.used += nb

    def in_hop(d, slot):
        return pltpu.make_async_remote_copy(
            src_ref=r.d_attn.at[d, pl.ds(0, half), :],
            dst_ref=r.gin.at[mine, own_lane],
            send_sem=r.send.at[base_in + d],
            recv_sem=r.recv.at[base_in + slot],
            device_id={"b": jnp.int32(d)},
            device_id_type=MESH,
        )

    drain(attn_copies)
    for i in range(nb):
        d_in = mixer_in.total(i, 0)
        r_col = r.ids[i, mine, 0:1]
        inner = jnp.where(
            c == 0, inner_columns[:half, i : i + 1], inner_columns[half:, i : i + 1]
        )
        x = r.xc[i, mine, :].astype(f32)
        scaled = d_in * r_col
        grad = r.d_hidden[i] + scaled * gain_in - x * (r_col * r_col * inner / model)
        attn_part = attn_part + jnp.sum(scaled * x, axis=0, keepdims=True)
        r.d_attn[i, :half, :] = grad.astype(bf16)

        @pl.when(b == i)
        def _():
            r.gin[mine, own_lane] = r.d_attn[i, :half, :]

        @pl.when(b != i)
        def _():
            in_hop(i, b).start()

    r.extra_own[...] = jnp.where(which_row == experts + 2, attn_part, r.extra_own[...])
    tail_copy = ship(r.extra_own, r.extra_in, core)
    tail_copy.wait_recv()
    shared = (which_row == experts + 1) | (which_row == experts + 2)
    r.tail_all[a] = r.extra_own[...] + jnp.where(shared, r.extra_in[...], 0.0)
    r.tail_all[a, experts + 3 : experts + 5, 0:head] = sums[4:6, 0:head]
    tail_copies = over_a(r.tail_all.at[a], r.tail_all)
    out_y = lanes_onward(out_copies, fourth, across)
    in_more = []
    for k in range(1, nb):
        place = lax.rem(b + k, nb)
        lane = lane_of(place)
        pltpu.make_async_remote_copy(
            src_ref=r.gin.at[mine, lane],
            dst_ref=r.gin.at[mine, lane],
            send_sem=r.send.at[base_in + place],
            recv_sem=r.recv.at[base_in + place],
            device_id=core,
            device_id_type=MESH,
        ).wait_recv()
        in_more.append(ship(r.gin.at[mine, lane], r.gin.at[mine, lane], core))
    in_more.append(ship(r.gin.at[mine, own_lane], r.gin.at[mine, own_lane], core))
    out_more = lanes_onward(out_y, mine, core)
    block = r.block_out.at[mine, own_lane]
    out_more.append(ship(block, block, core))
    arrive(pending)
    for j in range(4):
        mine_here = r.gsend[j, a] if j < 3 else r.gout[a]
        total = mine_here.astype(f32)
        for k in range(na - 1):
            came = r.gin_w[j, k] if j < 3 else r.gout_in[k]
            total = total + came.astype(f32)
        r.proj[j] = total
    results.append(move(r.proj, r.proj_out))
    arrive(out_more)
    results.append(move(r.block_out, r.out_rows))
    arrive(tail_copies)
    r.tail[...] = jnp.sum(r.tail_all[...], axis=0)
    arrive(in_more)
    results.append(move(r.gin, r.in_rows))
    mixer_in.finish()
    mixer.finish((1,))
    for line in [heads_sum, pay_line] + act_lines + cd_sums + ho_lines + q_lines + kv_lines:
        line.finish()
    for d in range(nb):

        @pl.when(b != d)
        def _():
            in_hop(d, b).wait_send()

    drain(list(sent))
    for copy in results:
        copy.wait()
    assert net.used <= r.send.shape[0] and local_used[0] <= r.local.shape[0]


def layer(sizes, dims, ins):
    nb, na, head, heads, experts, ff, top = dims
    tok, model = ins[0].shape
    part, col, half = model // nb, nb * tok, tok // 2
    sub, width, wide = part // na, heads * head, experts * ff
    others = max(na - 1, 1)
    shape = jax.ShapeDtypeStruct
    vmem, hbm = pl.BlockSpec(memory_space=pltpu.VMEM), pl.BlockSpec(memory_space=pl.ANY)
    outs = [
        shape((tok, model), bf16),
        shape((tok, model), bf16),
        shape((sub, wide), bf16),
        shape((sub, wide), bf16),
        shape((sub, wide), bf16),
        shape((others, sub, wide), bf16),
        shape((others, sub, wide), bf16),
        shape((others, sub, wide), bf16),
        shape((4, sub, width), f32),
        shape((16, part), f32),
    ]
    work = dict(
        xc=((nb, tok, part), bf16),
        cotc=((nb, tok, part), bf16),
        rows_all=((na, nb, 8, tok), f32),
        rows_own=((8, tok), f32),
        cols_own=((16, sub), f32),
        cols_all=((na, 16, sub), f32),
        cols_sum=((16, part), f32),
        wqkv=((3, na, sub, width), bf16),
        wo=((na, sub, width), bf16),
        wg=((na, sub, wide), bf16),
        wu=((na, sub, wide), bf16),
        wd=((na, sub, wide), bf16),
        stage=((sub, experts, ff), bf16),
        hn=((nb, tok, part), bf16),
        raw=((col, 3 * head), f32),
        q_rot=((col, head), bf16),
        kv=((na, col, 2 * head), bf16),
        stat=((col, 128), f32),
        ho=((col, width), bf16),
        cos_tab=((col, head), f32),
        sin_tab=((col, head), f32),
        pkv=((nb, col, 2 * head), bf16),
        gkv=((nb, col, 2 * head), bf16),
        pq=((nb, col, head), bf16),
        gq=((nb, col, head), bf16),
        pcd=((top, nb, ff // head * tok, head), bf16),
        gcd=((top, nb, ff // head * tok, head), bf16),
        acc=((nb, half, part), f32),
        sendc=((nb, half, 2 * part), bf16),
        recvc=((nb, half, 2 * part), bf16),
        sendy=((nb, half, 2 * part), bf16),
        recvy=((nb, half, 2 * part), bf16),
        hidden=((nb, half, part), f32),
        d_hidden=((nb, half, part), f32),
        scaled=((nb, tok, part), bf16),
        small=((nb, 16, tok), f32),
        small_in=((nb, 16, tok), f32),
        pay=((nb, tok, 3 * top * ff), bf16),
        wide=((3, col, width), bf16),
        pair=((4, 8, tok), f32),
        late_small=((nb, 16, tok), f32),
        extra_own=((16, part), f32),
        extra_in=((16, part), f32),
        d_attn=((nb, tok, part), bf16),
        out_half=((nb, half, part), bf16),
        block_out=((tok, model), bf16),
        head_acc=((col, head), f32),
        dkv_acc=((col, 2 * head), f32),
        dkv_send=((others, col, 2 * head), bf16),
        dkv_in=((others, col, 2 * head), bf16),
        gsend=((3, na, sub, width), bf16),
        gin_w=((3, others, sub, width), bf16),
        gout=((na, sub, width), bf16),
        gout_in=((others, sub, width), bf16),
        gin=((tok, model), bf16),
        s4=((4 * nb, 8, tok), f32),
        gain_acc=((8, head), f32),
        tail_all=((na, 16, part), f32),
        ids=((nb, tok, 8), f32),
        gains=((8, head), f32),
        docs=((na, 1, col), f32),
        proj=((4, sub, width), f32),
    )
    count = 174 + 26 * na
    scratch = [pltpu.VMEM(*work[name]) for name in WORK[:-3]] + [
        pltpu.SemaphoreType.DMA((count,)),
        pltpu.SemaphoreType.DMA((count,)),
        pltpu.SemaphoreType.DMA((15,)),
    ]
    return pl.pallas_call(
        functools.partial(layer_kernel, sizes, dims),
        out_shape=outs,
        in_specs=[hbm] * 9 + [vmem] * 8,
        out_specs=[hbm] * 9 + [vmem],
        scratch_shapes=scratch,
        compiler_params=pltpu.CompilerParams(
            collective_id=1, has_side_effects=True, vmem_limit_bytes=67043328
        ),
        name="layer",
    )(*ins)


def last_kernel(experts, ff, sub, *refs):
    out_rows, in_rows, owns, cames, proj = refs[0], refs[1], refs[2:5], refs[5:8], refs[8]
    tail, refs = refs[9], refs[10:]
    block_out, grad_in, grads, projections = refs[0], refs[1], refs[2:5], refs[5:9]
    router, gain_attn, gain_ffn, gain_q, gain_k = refs[9:]
    step = 32

    @pl.loop(0, block_out.shape[0] // step)
    def _(n):
        rows = pl.ds(pl.multiple_of(n * step, step), step)
        block_out[rows, :] = out_rows[rows, :]
        grad_in[rows, :] = in_rows[rows, :].astype(f32)

    @pl.loop(0, owns[0].shape[0] // step)
    def _(n):
        rows = pl.ds(pl.multiple_of(n * step, step), step)
        for own, came, grad in zip(owns, cames, grads):
            for e in range(experts):
                lane = slice(e * ff, (e + 1) * ff)
                total = own[rows, lane].astype(f32)
                for k in range(came.shape[0]):
                    total = total + came[k, rows, lane].astype(f32)
                grad[rows, e, :] = total
        for j in range(4):
            projections[j][rows, :] = proj[j, rows, :]

    @pl.when(pl.program_id(0) == 0)
    def _():
        a = lax.axis_index("a")
        piece = tail[:, :sub]
        for k in range(1, tail.shape[1] // sub):
            piece = jnp.where(a == k, tail[:, k * sub : (k + 1) * sub], piece)
        router[...] = piece[:experts]
        gain_ffn[...] = piece[experts + 1 : experts + 2]
        gain_attn[...] = piece[experts + 2 : experts + 3]
        gain_q[...] = tail[experts + 3 : experts + 4, : gain_q.shape[1]]
        gain_k[...] = tail[experts + 4 : experts + 5, : gain_k.shape[1]]


def last(dims, ins):
    nb, na, head, heads, experts, ff, top = dims
    tok, model = ins[0].shape
    sub, wide = ins[2].shape
    others, width = ins[5].shape[0], ins[8].shape[2]
    steps = 2
    shape = jax.ShapeDtypeStruct
    rows = pl.BlockSpec((tok // steps, model), lambda i: (i, 0))
    own = pl.BlockSpec((sub // steps, wide), lambda i: (i, 0))
    came = pl.BlockSpec((others, sub // steps, wide), lambda i: (0, i, 0))
    grad = pl.BlockSpec((sub // steps, experts, ff), lambda i: (i, 0, 0))
    flat = pl.BlockSpec((sub // steps, width), lambda i: (i, 0))
    small = [shape((experts, sub), f32), shape((1, sub), f32), shape((1, sub), f32)]
    small += [shape((1, head), f32)] * 2
    return pl.pallas_call(
        functools.partial(last_kernel, experts, ff, sub),
        grid=(steps,),
        out_shape=[shape((tok, model), bf16), shape((tok, model), f32)]
        + [shape((sub, experts, ff), f32)] * 3
        + [shape((sub, width), f32)] * 4
        + small,
        in_specs=[rows, rows] + [own] * 3 + [came] * 3
        + [pl.BlockSpec((4, sub // steps, width), lambda i: (0, i, 0))]
        + [pl.BlockSpec(ins[9].shape, lambda i: (0, 0))],
        out_specs=[rows, rows] + [grad] * 3 + [flat] * 4
        + [pl.BlockSpec(item.shape, lambda i: (0, 0)) for item in small],
        name="last",
    )(*ins)


def on_device(
    sizes,
    tokens_in,
    doc_ids,
    expert_ids,
    attn_gain,
    q_gain,
    k_gain,
    w_query,
    w_key,
    w_value,
    w_output,
    ffn_gain,
    w_router,
    w_gate,
    w_up,
    w_down,
    cotangent,
):
    nb, na = sizes["b"], sizes["a"]
    tok, model = tokens_in.shape
    part = model // nb
    sub = part // na
    head = q_gain.shape[0]
    width = w_query.shape[1]
    heads = width // head
    experts, ff = w_gate.shape[1], w_gate.shape[2]
    top = expert_ids.shape[1]
    dims = (nb, na, head, heads, experts, ff, top)

    speed = theta ** (-2.0 * (np.arange(head) % (head // 2)) / head)
    parts = layer(
        sizes,
        dims,
        [
            tokens_in, cotangent, w_query, w_key, w_value, w_output, w_gate, w_up, w_down,
            expert_ids.T, doc_ids[None], w_router.T, attn_gain, ffn_gain, q_gain[None],
            k_gain[None], jnp.asarray(speed, f32)[None],
        ],
    )
    (
        block_out, grad_in, grad_gate, grad_up, grad_down, grad_query, grad_key, grad_value,
        grad_output, router, gain_attn, gain_ffn, gain_q, gain_k,
    ) = last(dims, parts)
    return (
        block_out,
        grad_in,
        gain_attn.reshape(sub),
        gain_q.reshape(head),
        gain_k.reshape(head),
        grad_query,
        grad_key,
        grad_value,
        grad_output,
        gain_ffn.reshape(sub),
        router.T,
        grad_gate,
        grad_up,
        grad_down,
    )


def solution(mesh):
    cp, tp = mesh.shape["cp"], mesh.shape["tp"]
    sizes = {"b": 4, "a": cp // 4, "y": 2, "c": tp // 2}
    split = Mesh(mesh.devices.reshape([sizes[axis] for axis in AXES]), AXES)
    cp, tp = ("b", "a"), ("y", "c")
    return jax.shard_map(
        functools.partial(on_device, sizes),
        mesh=split,
        in_specs=(
            P(cp, None),
            P(cp),
            P(cp, None),
            P(cp),
            P(),
            P(),
            P(cp, tp),
            P(cp, tp),
            P(cp, tp),
            P(cp, tp),
            P(cp),
            P(cp, None),
            P(cp, None, tp),
            P(cp, None, tp),
            P(cp, None, tp),
            P(cp, None),
        ),
        out_specs=(
            P(cp, None),
            P(cp, None),
            P(cp),
            P(),
            P(),
            P(cp, tp),
            P(cp, tp),
            P(cp, tp),
            P(cp, tp),
            P(cp),
            P(cp, None),
            P(cp, None, tp),
            P(cp, None, tp),
            P(cp, None, tp),
        ),
        check_vma=False,
    )
```

profile of v0, /device:TPU:0, one launch (start us, length us, event | category | flops | bytes accessed | tf_op | source)
XLA Modules:
  0.0 317.8 jit_solution(5468880460529012489)
XLA Ops:
  0.7 308.9 %layer.1 = (bf16[256,2048]{1,0:T(8,128)(2,1)}, bf16[256,2048]{1,0:T(8,128)(2,1)}, bf16[256,2048]{1,0:T(8,128)(2,1)}, bf16[256,2048]{1,0:T(8,128)(2,1)}, bf16[256...) custom-call(bf16[256,2048]{1,0:T(8,128)(2,1)} %refs_0_.1, ...), custom_call_target="tpu_custom_call" | custom-call | tf_op jit(solution)/shard_map/layer/pallas_call | solution.py:1197
  309.5 8.1 %last.1 = (bf16[256,2048]{1,0:T(8,128)(2,1)}, f32[256,2048]{1,0:T(8,128)}, f32[256,8,256]{2,1,0:T(8,128)}, f32[256,8,256]{2,1,0:T(8,128)}, f32[256,8,256]{2,1,0:...) custom-call(bf16[256,2048]{1,0:T(8,128)(2,1)} %get-tuple-element.38., ...), custom_call_target="tpu_custom_call" | custom-call | tf_op jit(solution)/shard_map/last/pallas_call | solution.py:1263
where the time goes:
time: 318 us
  Pallas kernels  317 us (100%)
    pallas_call x1, Pallas kernels, layer(): pl.pallas_call(functools.partial(layer_kernel, sizes, dims), out_shape=ou...  309 us
    pallas_call x1, Pallas kernels, last(): pl.pallas_call(functools.partial(last_kernel, experts, ff, sub), grid=(st...  8.05 us

commit v1 on v0

--- a/solution.py
+++ b/solution.py
@@ -59,29 +59,30 @@
             result = jnp.where(self.me["b"] == i, values[i], result)
         return result
 
-    def reduce(self, *args):
-        return Reduce(self, *args)
+    def reduce(self, *args, **options):
+        return Reduce(self, *args, **options)
 
     def spread(self, *blocks, start=True):
         return Spread(self, blocks, start)
 
 
 class Reduce:
-    def __init__(self, net, parts, got, make=None):
-        self.net, self.parts, self.got = net, parts, got
+    def __init__(self, net, parts, got, make=None, pieces=1):
+        self.net, self.parts, self.got, self.pieces = net, parts, got, pieces
         self.b = b = net.me["b"]
         self.base = net.used
-        net.used += 4
+        self.rows = parts.shape[1] // pieces
+        net.used += 4 * pieces
         self.order = [3 - b, net.pick(2, 0, 3, 1), net.pick(1, 3, 0, 2)]
         if make is None:
             for k in range(2):
-                self.hop(self.order[k]).start()
+                self.start(self.order[k])
             return
         if net.sizes["a"] > 2:
             for k in range(3):
                 make(self.order[k])
                 if k < 2:
-                    self.hop(self.order[k]).start()
+                    self.start(self.order[k])
             return
 
         @pl.loop(0, 3)
@@ -91,56 +92,65 @@
 
             @pl.when(k < 2)
             def _():
-                self.hop(d).start()
-
-    def hop(self, d):
+                self.start(d)
+
+    def start(self, d):
+        for p in range(self.pieces):
+            self.hop(d, p).start()
+
+    def piece(self, p):
+        return pl.ds(p * self.rows, self.rows)
+
+    def hop(self, d, p):
         net, b = self.net, self.b
         far = ((b == 0) & (d == 3)) | ((b == 3) & (d == 0))
         beside = jnp.where(b == 0, 1, 2)
         target, slot = jnp.where(far, beside, d), jnp.where(far, beside, b)
         return pltpu.make_async_remote_copy(
-            src_ref=self.parts.at[d],
-            dst_ref=self.got.at[slot],
-            send_sem=net.send.at[self.base + d],
-            recv_sem=net.recv.at[self.base + slot],
+            src_ref=self.parts.at[d, self.piece(p), :],
+            dst_ref=self.got.at[slot, self.piece(p), :],
+            send_sem=net.send.at[self.base + 4 * p + d],
+            recv_sem=net.recv.at[self.base + 4 * p + slot],
             device_id={"b": target},
             device_id_type=MESH,
         )
 
-    def came(self, i):
+    def came(self, i, p):
         net = self.net
+        block = self.got.at[i, self.piece(p), :]
         return pltpu.make_async_remote_copy(
-            src_ref=self.got.at[i],
-            dst_ref=self.got.at[i],
-            send_sem=net.send.at[self.base + i],
-            recv_sem=net.recv.at[self.base + i],
+            src_ref=block,
+            dst_ref=block,
+            send_sem=net.send.at[self.base + 4 * p + i],
+            recv_sem=net.recv.at[self.base + 4 * p + i],
             device_id=net.near(b=1),
             device_id_type=MESH,
         )
 
     def inner(self):
         b, d = self.b, self.order[2]
-
-        @pl.when((b == 1) | (b == 2))
-        def _():
-            self.came(b).wait_recv()
-            rows = self.parts.shape[1]
-            step = 256 if rows % 256 == 0 else rows
-
-            @pl.loop(0, rows // step)
-            def _(i):
-                sl = pl.ds(pl.multiple_of(i * step, step), step)
-                total = self.parts[d, sl, :].astype(f32) + self.got[b, sl, :].astype(f32)
-                self.parts[d, sl, :] = total.astype(bf16)
-
-        self.hop(d).start()
+        for p in range(self.pieces):
+
+            @pl.when((b == 1) | (b == 2))
+            def _():
+                self.came(b, p).wait_recv()
+                step = 256 if self.rows % 256 == 0 else self.rows
+
+                @pl.loop(0, self.rows // step)
+                def _(i):
+                    sl = pl.ds(pl.multiple_of(p * self.rows + i * step, step), step)
+                    total = self.parts[d, sl, :].astype(f32) + self.got[b, sl, :].astype(f32)
+                    self.parts[d, sl, :] = total.astype(bf16)
+
+            self.hop(d, p).start()
 
     def wait(self):
         for i in range(4):
 
             @pl.when((self.b != i) & (jnp.abs(self.b - i) <= 2))
             def _():
-                self.came(i).wait_recv()
+                for p in range(self.pieces):
+                    self.came(i, p).wait_recv()
 
     def total(self, *index):
         b = self.b
@@ -155,7 +165,8 @@
 
             @pl.when(self.b != d)
             def _():
-                self.hop(d).wait_send()
+                for p in range(self.pieces):
+                    self.hop(d, p).wait_send()
 
 
 class Spread:
@@ -481,7 +492,7 @@
                 piece = term[:, h * head : (h + 1) * head]
                 r.pkv[h, rows_of(i), (j - 1) * head : j * head] = piece
 
-    kv_sum = net.reduce(r.pkv, r.gkv)
+    kv_sum = net.reduce(r.pkv, r.gkv, pieces=2)
     cot_y = onward(cot_copies, r.cotc, fourth, across)
     arrive(q_weights)
 
@@ -664,7 +675,7 @@
 
             chosen(r.scaled[d], w, d, put)
 
-    gu_sum = net.reduce(r.pkv, r.gkv, make)
+    gu_sum = net.reduce(r.pkv, r.gkv, make, pieces=2)
     gu_sum.inner()
     make(b)
     arrive(small_copies)
@@ -820,7 +831,7 @@
         for h in range(heads):
             r.pq[h, rows_of(i), :] = term[:, h * head : (h + 1) * head]
 
-    heads_sum = net.reduce(r.pq, r.gq)
+    heads_sum = net.reduce(r.pq, r.gq, pieces=2)
 
     expert_grad(1, r.scaled, r.wg, 1)
     pending += half_to_a(r.wg, r.gate_in, 1)
@@ -947,11 +958,11 @@
     s4_copies = [ship(r.s4.at[place16], r.s4.at[place16], place) for place in group]
 
     def kv_piece(s):
-        return net.spread(
-            lambda i: head_block(r.wide.at[1], i, s * tok, tok),
-            lambda i: head_block(r.wide.at[2], i, s * tok, tok),
-            start=s < 2,
-        )
+        def block(i):
+            lane = pl.ds(pl.multiple_of(i * head, head), head)
+            return r.wide.at[pl.ds(1, 2), pl.ds(s * tok, tok), lane]
+
+        return net.spread(block, start=s < 2)
 
     kv_lines = [kv_piece(s) for s in range(nb)]
     def weight_grad(j):
@@ -1188,7 +1199,7 @@
         docs=((na, 1, col), f32),
         proj=((4, sub, width), f32),
     )
-    count = 174 + 26 * na
+    count = 170 + 26 * na
     scratch = [pltpu.VMEM(*work[name]) for name in WORK[:-3]] + [
         pltpu.SemaphoreType.DMA((count,)),
         pltpu.SemaphoreType.DMA((count,)),

time: 318 us -> 319 us (level)
  no operation moved by 1% of the time
where the time goes in v1:
time: 319 us; the launch traced here: 317 us
  Pallas kernels  316 us (99%)
    pallas_call x1, Pallas kernels, layer(): pl.pallas_call(functools.partial(layer_kernel, sizes, dims), out_shape=ou...  308 us
    pallas_call x1, Pallas kernels, last(): pl.pallas_call(functools.partial(last_kernel, experts, ff, sub), grid=(st...  8.05 us

profile of v1, /device:TPU:0, one launch (start us, length us, event | category | flops | bytes accessed | tf_op | source)
XLA Modules:
  0.0 317.2 jit_solution(6900223042475965022)
XLA Ops:
  0.7 308.3 %layer.1 = (bf16[256,2048]{1,0:T(8,128)(2,1)}, bf16[256,2048]{1,0:T(8,128)(2,1)}, bf16[256,2048]{1,0:T(8,128)(2,1)}, bf16[256,2048]{1,0:T(8,128)(2,1)}, bf16[256...) custom-call(bf16[256,2048]{1,0:T(8,128)(2,1)} %refs_0_.1, ...), custom_call_target="tpu_custom_call" | custom-call | tf_op jit(solution)/shard_map/layer/pallas_call | solution.py:1208
  309.0 8.1 %last.1 = (bf16[256,2048]{1,0:T(8,128)(2,1)}, f32[256,2048]{1,0:T(8,128)}, f32[256,8,256]{2,1,0:T(8,128)}, f32[256,8,256]{2,1,0:T(8,128)}, f32[256,8,256]{2,1,0:...) custom-call(bf16[256,2048]{1,0:T(8,128)(2,1)} %get-tuple-element.38., ...), custom_call_target="tpu_custom_call" | custom-call | tf_op jit(solution)/shard_map/last/pallas_call | solution.py:1274

commit v2 on v0

--- a/solution.py
+++ b/solution.py
@@ -947,11 +947,11 @@
     s4_copies = [ship(r.s4.at[place16], r.s4.at[place16], place) for place in group]
 
     def kv_piece(s):
-        return net.spread(
-            lambda i: head_block(r.wide.at[1], i, s * tok, tok),
-            lambda i: head_block(r.wide.at[2], i, s * tok, tok),
-            start=s < 2,
-        )
+        def block(i):
+            lane = pl.ds(pl.multiple_of(i * head, head), head)
+            return r.wide.at[pl.ds(1, 2), pl.ds(s * tok, tok), lane]
+
+        return net.spread(block, start=s < 2)
 
     kv_lines = [kv_piece(s) for s in range(nb)]
     def weight_grad(j):
@@ -1188,7 +1188,7 @@
         docs=((na, 1, col), f32),
         proj=((4, sub, width), f32),
     )
-    count = 174 + 26 * na
+    count = 158 + 26 * na
     scratch = [pltpu.VMEM(*work[name]) for name in WORK[:-3]] + [
         pltpu.SemaphoreType.DMA((count,)),
         pltpu.SemaphoreType.DMA((count,)),

time: 318 us -> 318 us (level)
  no operation moved by 1% of the time
where the time goes in v2:
time: 318 us
  Pallas kernels  317 us (100%)
    pallas_call x1, Pallas kernels, layer(): pl.pallas_call(functools.partial(layer_kernel, sizes, dims), out_shape=ou...  309 us
    pallas_call x1, Pallas kernels, last(): pl.pallas_call(functools.partial(last_kernel, experts, ff, sub), grid=(st...  8.05 us

profile of v2, /device:TPU:0, one launch (start us, length us, event | category | flops | bytes accessed | tf_op | source)
XLA Modules:
  0.0 317.5 jit_solution(7283365858645882389)
XLA Ops:
  0.7 308.6 %layer.1 = (bf16[256,2048]{1,0:T(8,128)(2,1)}, bf16[256,2048]{1,0:T(8,128)(2,1)}, bf16[256,2048]{1,0:T(8,128)(2,1)}, bf16[256,2048]{1,0:T(8,128)(2,1)}, bf16[256...) custom-call(bf16[256,2048]{1,0:T(8,128)(2,1)} %refs_0_.1, ...), custom_call_target="tpu_custom_call" | custom-call | tf_op jit(solution)/shard_map/layer/pallas_call | solution.py:1197
  309.3 8.1 %last.1 = (bf16[256,2048]{1,0:T(8,128)(2,1)}, f32[256,2048]{1,0:T(8,128)}, f32[256,8,256]{2,1,0:T(8,128)}, f32[256,8,256]{2,1,0:T(8,128)}, f32[256,8,256]{2,1,0:...) custom-call(bf16[256,2048]{1,0:T(8,128)(2,1)} %get-tuple-element.38., ...), custom_call_target="tpu_custom_call" | custom-call | tf_op jit(solution)/shard_map/last/pallas_call | solution.py:1263
